TPU v7x, 32 devices: a whole 2x2x4 slice. The times are simulated.
32 devices in a mesh: lat: 4 (over y, x), lon: 8 (over z, core).
Axes of the slice: x: 2, y: 2, z: 4, core: 2. Of those that a mesh axis runs over, the one named last changes fastest.
Arguments:
- right_side: float32 [8, 768, 1024], P(None, 'lat', 'lon'), may hold values from -16 to 16
- center: float32 [768, 1024], P('lat', 'lon'), may hold values from 3.7 to 5.5
- couplings: float32 [4, 768, 1024], P(None, 'lat', 'lon'), may hold values from 0.15 to 0.45
- land_sea: int32 [768, 1024], P('lat', 'lon'), may hold values 0 or 1
- fold_partner: int32 [1024], replicated, may hold values from 0 to 1023, as said below
Outputs:
- solution: float32 [8, 768, 1024], P(None, 'lat', 'lon')
- residual: float32 [8, 768, 1024], P(None, 'lat', 'lon')
Inputs may be any that keep to these rules, and one draw needn't show every extreme that they name: fold_partner[i] = (s - i) mod 1024 for one integer s, so fold_partner[fold_partner[i]] = i.
All inputs are finite; a program needn't handle non-finite values. No bound on the sum of `land_sea` on one device may be relied on, other than what follows from the above.
Results may differ from a plain program's by a relative error of at most 0.0003.
Values sent between devices are 32-bit elements; how exact they have to be, the bound alone decides.
No kernel may reach another device: no remote copies, remote signals or barrier semaphores. Data moves between devices by JAX's collectives and lax.ppermute only.
A program may use at most 64 MiB of HBM per device.

v0:
```python
import jax
import jax.numpy as jnp
from jax import lax
from jax.experimental import pallas as pl
from jax.experimental.pallas import tpu as pltpu
from jax.sharding import PartitionSpec as P

ITERS = 3
DEPTH = ITERS
SUB = 8
TOP = 2 * SUB


def pack_kernel(
    rhs, center, couplings, land, east, west, north, south, scaled, weights, edges, scale, mask, arrivals
):
    members = rhs.shape[0]
    fields = members + couplings.shape[0] + 1
    rows, cols = center.shape
    lane = lax.broadcasted_iota(jnp.int32, (SUB, cols), 1)
    group = 2 * DEPTH
    pairs = ((land, mask), (center, scale), (rhs, scaled), (couplings, edges))
    copies = [pltpu.make_async_copy(a, b, arrivals.at[i]) for i, (a, b) in enumerate(pairs)]
    for copy in copies:
        copy.start()
    for copy in copies:
        copy.wait()

    def step(index, carry):
        at = pl.multiple_of(index * SUB, SUB)
        here = pl.ds(at, SUB)
        weight = mask[here, :].astype(jnp.float32) / scale[here, :]
        weights[here, :] = weight
        values = []
        for m in range(members):
            value = scaled[m, here, :] * weight
            scaled[m, here, :] = value
            values.append(value)
        values += [edges[c, here, :] for c in range(edges.shape[0])]
        values.append(weight)
        to_east = jnp.zeros((SUB, cols), jnp.float32)
        to_west = jnp.zeros((SUB, cols), jnp.float32)
        for f, value in enumerate(values):
            base = group * f
            moved = pltpu.roll(value, (base + DEPTH) % cols, 1)
            pick_east = jnp.logical_and(lane >= base, lane < base + DEPTH)
            pick_west = jnp.logical_and(lane >= base + DEPTH, lane < base + group)
            to_east = jnp.where(pick_east, moved, to_east)
            to_west = jnp.where(pick_west, moved, to_west)
        east[here, :] = to_east
        west[here, :] = to_west
        return carry

    lax.fori_loop(0, rows // SUB, step, 0, unroll=2)
    copies = north.shape[0]
    for ref, at in ((north.at[0], rows - DEPTH), (south, 0)):
        span = slice(at, at + DEPTH)
        for f in range(fields):
            if f < members:
                value = scaled[f, span, :]
            elif f < fields - 1:
                value = edges[f - members, span, :]
            else:
                value = weights[span, :]
            ref[DEPTH * f : DEPTH * (f + 1), :] = value
        used = DEPTH * fields
        ref[used:, :] = jnp.zeros((ref.shape[0] - used, cols), jnp.float32)
    top = north[0]
    for b in range(1, copies):
        north[b] = top


def stencil_kernel(
    partner, scaled, weights, couplings, center, from_west, from_east, from_north, from_south, ring,
    first, second, third, moments, held, coeff, level_one, level_two,
):
    members = scaled.shape[0]
    edges = couplings.shape[0]
    fields = members + edges + 1
    rows, cols = center.shape
    group = 2 * DEPTH
    wide = 2 * cols
    blocks = ring.shape[0]
    packed = ring.shape[1]
    f_east, f_north, f_ne, f_nw, f_weight = (members + c for c in range(5))
    lat_last = lax.axis_index("lat") == lax.axis_size("lat") - 1
    first_col = lax.axis_index("lon") * cols
    lane = lax.broadcasted_iota(jnp.int32, (SUB, cols), 1)
    in_west = lane % group < DEPTH
    bottom = TOP + rows

    zeros = jnp.zeros((SUB, wide), jnp.float32)
    for at in (0, SUB, bottom, bottom + SUB):
        for f in range(fields):
            held[f, at : at + SUB, :] = zeros
    for at in (0, bottom + SUB):
        for m in range(members):
            level_one[m, at : at + SUB, :] = zeros
            level_two[m, at : at + SUB, :] = zeros

    def spread(value, f):
        return pltpu.roll(value, (cols - group * f - DEPTH) % cols, 1)

    def fill(index, carry):
        at = pl.multiple_of(index * SUB, SUB)
        to = pl.multiple_of(index * SUB + TOP, SUB)
        side = jnp.where(in_west, from_west[pl.ds(at, SUB), :], from_east[pl.ds(at, SUB), :])
        for f in range(fields):
            if f < members:
                value = scaled[f, pl.ds(at, SUB), :]
            elif f < f_weight:
                value = couplings[f - members, pl.ds(at, SUB), :]
            else:
                value = weights[pl.ds(at, SUB), :]
            held[f, pl.ds(to, SUB), :cols] = value
            held[f, pl.ds(to, SUB), cols:] = spread(side, f)
        return carry

    lax.fori_loop(0, rows // SUB, fill, 0)

    side_south = from_south[packed : packed + SUB, :]
    for f in range(fields):
        held[f, TOP - DEPTH : TOP, :cols] = from_south[DEPTH * f : DEPTH * (f + 1), :]
        held[f, TOP - DEPTH : TOP, cols:] = spread(side_south, f)[SUB - DEPTH :, :]

    @pl.when(jnp.logical_not(lat_last))
    def _():
        side_north = from_north[packed : packed + SUB, :]
        for f in range(fields):
            held[f, bottom : bottom + DEPTH, :cols] = from_north[DEPTH * f : DEPTH * (f + 1), :]
            held[f, bottom : bottom + DEPTH, cols:] = spread(side_north, f)[:DEPTH, :]

    @pl.when(lat_last)
    def _():
        total = blocks * cols
        shift = cols.bit_length() - 1
        row = lax.broadcasted_iota(jnp.int32, (packed, cols), 0)
        spot = lax.broadcasted_iota(jnp.int32, (packed, cols), 1)

        def of(f):
            return jnp.logical_and(row >= DEPTH * f, row < DEPTH * (f + 1))

        offset = jnp.where(jnp.logical_or(of(f_east), of(f_ne)), -1, jnp.where(of(f_nw), 1, 0))
        beside = jnp.where(spot < cols // 2, spot + cols, spot - cols)
        mirrored = []
        for column in (spot, beside):
            source = partner[0] - first_col + offset - column
            source = jnp.where(source < 0, source + total, source)
            source = jnp.where(source < 0, source + total, source)
            source = jnp.where(source >= total, source - total, source)
            block = lax.shift_right_logical(source, shift)
            place = jnp.bitwise_and(source, cols - 1)
            found = jnp.zeros((packed, cols), jnp.float32)
            for b in range(blocks):
                taken = jnp.take_along_axis(ring[b], place, axis=1, mode="promise_in_bounds")
                found = jnp.where(block == b, taken, found)
            mirrored.append(found)
        for half, found in enumerate(mirrored):
            lanes = slice(half * cols, (half + 1) * cols)
            for f in range(fields):
                back = 2 if f in (f_north, f_ne, f_nw) else 1
                for k in range(DEPTH):
                    at = DEPTH - back - k
                    if at >= 0:
                        spot_row = DEPTH * f + at
                        held[f, bottom + k : bottom + k + 1, lanes] = found[spot_row : spot_row + 1, :]
            top = slice(bottom - 1, bottom)
            across = found[DEPTH * f_north + DEPTH - 1 : DEPTH * (f_north + 1), :]
            held[f_north, top, lanes] = 0.5 * (held[f_north, top, lanes] + across)
            held[f_ne, top, lanes] = jnp.zeros((1, cols), jnp.float32)
            held[f_nw, top, lanes] = jnp.zeros((1, cols), jnp.float32)

    def east_of(value):
        return pltpu.roll(value, wide - 1, 1)

    def west_of(value):
        return pltpu.roll(value, 1, 1)

    def around(ref, at):
        return ref.at[:, pl.ds(pl.multiple_of(at - SUB, SUB), 3 * SUB), :]

    def make_coeff(index, carry):
        at = pl.multiple_of(index * SUB, SUB)
        here = pl.ds(at, SUB)
        near = around(held, at)
        weight = held[f_weight, here, :]
        weight_east = east_of(weight)
        weight_west = west_of(weight)
        coeff[0, here, :] = west_of(weight * held[f_east, here, :])
        coeff[1, here, :] = west_of(weight * held[f_ne, here, :])
        coeff[2, here, :] = weight_west * near[f_nw, SUB - 1 : 2 * SUB - 1, :]
        coeff[3, here, :] = weight_east * held[f_east, here, :]
        coeff[4, here, :] = east_of(weight * held[f_nw, here, :])
        coeff[5, here, :] = weight_east * near[f_ne, SUB - 1 : 2 * SUB - 1, :]
        coeff[6, here, :] = weight * held[f_north, here, :]
        coeff[7, here, :] = weight * near[f_north, SUB - 1 : 2 * SUB - 1, :]
        return carry

    wide_row = lax.broadcasted_iota(jnp.int32, (SUB, wide), 0)
    is_first = wide_row == 0
    is_last = wide_row == SUB - 1
    chunks = rows // SUB
    lax.fori_loop(1, chunks + 3, make_coeff, 0)

    def level(source, target, result):
        def chunk(index, carry, inside):
            at = pl.multiple_of(index * SUB, SUB)
            here = pl.ds(at, SUB)
            c = [coeff[k, here, :] for k in range(8)]
            if inside:
                inner = pl.ds(pl.multiple_of(at - TOP, SUB), SUB)
                scale = center[inner, :]
            sums = []
            after = pl.ds(pl.multiple_of(at + SUB, SUB), SUB)
            before = pl.ds(pl.multiple_of(at - SUB, SUB), SUB)
            for m in range(members):
                mid = source[m, here, :]
                up = pltpu.roll(jnp.where(is_first, source[m, after, :], mid), SUB - 1, 0)
                down = pltpu.roll(jnp.where(is_last, source[m, before, :], mid), 1, 0)
                new = c[6] * up + c[7] * down
                new = new + east_of(c[0] * mid + c[1] * up + c[2] * down)
                new = new + west_of(c[3] * mid + c[4] * up + c[5] * down)
                if target is not None:
                    target[m, here, :] = new
                if inside:
                    kept = new[:, :cols]
                    result[m, inner, :] = kept
                    scaled = scale * mid[:, :cols]
                    sums.append(carry[2 * m] + scaled * mid[:, :cols])
                    sums.append(carry[2 * m + 1] + scaled * kept)
            return tuple(sums) if inside else carry

        start = tuple(jnp.zeros((SUB, cols), jnp.float32) for _ in range(2 * members))
        if target is not None:
            chunk(1, 0, False)
        out = lax.fori_loop(2, chunks + 2, lambda i, s: chunk(i, s, True), start)
        if target is not None:
            chunk(chunks + 2, 0, False)
        return out

    totals = [level(held, level_one, first), level(level_one, level_two, second), level(level_two, None, third)]
    out_row = lax.broadcasted_iota(jnp.int32, (SUB, cols), 0)
    tile = jnp.zeros((SUB, cols), jnp.float32)
    for k in range(2 * DEPTH):
        gathered = jnp.zeros((SUB, cols), jnp.float32)
        for m in range(members):
            one = jnp.sum(totals[k // 2][2 * m + k % 2], axis=0, keepdims=True)
            gathered = jnp.where(out_row == m, one, gathered)
        tile = jnp.where(lane == k, jnp.sum(gathered, axis=1, keepdims=True), tile)
    for b in range(moments.shape[0]):
        moments[b] = tile


def combine_kernel(moments, zeroth, center, first, second, third, solution, residual):
    def inner(p, q):
        total = 0.0
        for i, a in enumerate(p):
            for j, b in enumerate(q):
                total = total + a * b * nu[i + j]
        return total

    parts = [moments[b] for b in range(moments.shape[0])]
    while len(parts) > 1:
        half = len(parts) // 2
        parts = [a + b for a, b in zip(parts[:half], parts[half : 2 * half])] + parts[2 * half :]
    summed = parts[0]
    nu = [summed[:, k : k + 1] for k in range(2 * DEPTH)]
    one = jnp.ones_like(nu[0])
    scaled = [one]
    direction = [one]
    answer = [jnp.zeros_like(one)] * DEPTH
    gamma = nu[0]
    for iteration in range(DEPTH):
        image = [d - e for d, e in zip(direction + [0.0], [0.0] + direction)]
        step = gamma / inner(direction, image)
        for i, d in enumerate(direction):
            answer[i] = answer[i] + step * d
        scaled = [z - step * q for z, q in zip(scaled + [0.0], image)]
        if iteration + 1 < DEPTH:
            gamma_next = inner(scaled, scaled)
            ratio = gamma_next / gamma
            direction = [z + ratio * d for z, d in zip(scaled, direction + [0.0])]
            gamma = gamma_next

    rows, cols = center.shape
    members = zeroth.shape[0]
    wide_answer = [jnp.broadcast_to(a, (members, cols)) for a in answer]
    wide_scaled = [jnp.broadcast_to(a, (members, cols)) for a in scaled]

    def chunk(index, carry):
        here = pl.ds(pl.multiple_of(index * SUB, SUB), SUB)
        scale = center[here, :]
        for m in range(members):
            basis = [zeroth[m, here, :], first[m, here, :], second[m, here, :], third[m, here, :]]
            got = sum(a[m : m + 1, :] * v for a, v in zip(wide_answer, basis))
            left = sum(a[m : m + 1, :] * v for a, v in zip(wide_scaled, basis))
            solution[m, here, :] = got
            residual[m, here, :] = scale * left
        return carry

    lax.fori_loop(0, rows // SUB, chunk, 0)


def shifted(value, axis, by, closed):
    count = lax.axis_size(axis)
    pairs = [(i, (i + by) % count) for i in range(count) if closed or 0 <= i + by < count]
    return lax.ppermute(value, axis, pairs)


def body(right_side, center, couplings, land_sea, fold_partner):
    members, rows, cols = right_side.shape
    fields = members + couplings.shape[0] + 1
    packed = -(-DEPTH * fields // SUB) * SUB
    f32 = jnp.float32
    vmem = pl.BlockSpec(memory_space=pltpu.VMEM)
    smem = pl.BlockSpec(memory_space=pltpu.SMEM)
    params = pltpu.CompilerParams(vmem_limit_bytes=32 * 1024 * 1024)

    def shape(*dims):
        return jax.ShapeDtypeStruct(dims, f32)

    lon_count = lax.axis_size("lon")
    devices = lon_count * lax.axis_size("lat")
    east, west, north, south, scaled, weights, edges, scale = pl.pallas_call(
        pack_kernel,
        in_specs=[pl.BlockSpec(memory_space=pltpu.HBM)] * 4,
        out_specs=[vmem] * 8,
        out_shape=[shape(rows, cols)] * 2
        + [shape(lon_count, packed, cols), shape(packed, cols)]
        + [shape(members, rows, cols), shape(rows, cols), shape(*couplings.shape), shape(rows, cols)],
        scratch_shapes=[pltpu.VMEM((rows, cols), jnp.int32), pltpu.SemaphoreType.DMA((4,))],
        compiler_params=params,
        name="pack",
    )(right_side, center, couplings, land_sea)

    from_west = shifted(east, "lon", 1, True)
    from_east = shifted(west, "lon", -1, True)
    ring = lax.all_to_all(north, "lon", 0, 0, tiled=False)
    north = north[0]
    in_west = (lax.broadcasted_iota(jnp.int32, (SUB, cols), 1) % (2 * DEPTH)) < DEPTH
    upper = jnp.where(in_west, from_west[rows - SUB :], from_east[rows - SUB :])
    lower = jnp.where(in_west, from_west[:SUB], from_east[:SUB])
    from_south = shifted(jnp.concatenate([north, upper]), "lat", 1, False)
    from_north = shifted(jnp.concatenate([south, lower]), "lat", -1, False)

    tall = rows + 2 * TOP
    first, second, third, moments = pl.pallas_call(
        stencil_kernel,
        in_specs=[smem] + [vmem] * 9,
        out_specs=[vmem] * 4,
        out_shape=[shape(members, rows, cols)] * 3 + [shape(devices, SUB, cols)],
        scratch_shapes=[
            pltpu.VMEM((fields, tall, 2 * cols), f32),
            pltpu.VMEM((8, tall, 2 * cols), f32),
            pltpu.VMEM((members, tall, 2 * cols), f32),
            pltpu.VMEM((members, tall, 2 * cols), f32),
        ],
        compiler_params=params,
        name="stencil",
    )(fold_partner, scaled, weights, edges, scale, from_west, from_east, from_north, from_south, ring)

    moments = lax.all_to_all(moments, ("lat", "lon"), 0, 0, tiled=False)

    return tuple(
        pl.pallas_call(
            combine_kernel,
            in_specs=[vmem] * 6,
            out_specs=[vmem] * 2,
            out_shape=[shape(members, rows, cols)] * 2,
            compiler_params=params,
            name="combine",
        )(moments, scaled, scale, first, second, third)
    )


def solution(mesh):
    return jax.shard_map(
        body,
        mesh=mesh,
        in_specs=(
            P(None, "lat", "lon"),
            P("lat", "lon"),
            P(None, "lat", "lon"),
            P("lat", "lon"),
            P(),
        ),
        out_specs=(P(None, "lat", "lon"), P(None, "lat", "lon")),
        check_vma=False,
    )
```

profile of v0, /device:TPU:0, one launch (start us, length us, event | category | flops | bytes accessed | tf_op | source)
XLA Modules:
  0.0 59.6 jit_solution(12954016927546086152)
XLA Ops:
  0.6 0.0 copy-start
  0.6 1.1 %copy-done = f32[8,192,128]{2,1,0:T(8,128)S(1)} copy-done((f32[8,192,128]{2,1,0:T(8,128)S(1)}, f32[8,192,128]{2,1,0:T(8,128)}, u32[]{:S(2)}) %copy-start) | copy-done | bytes 786456
  1.8 0.0 copy-start.1
  1.8 1.0 %copy-done.1 = f32[4,192,128]{2,1,0:T(8,128)S(1)} copy-done((f32[4,192,128]{2,1,0:T(8,128)S(1)}, f32[4,192,128]{2,1,0:T(8,128)}, u32[]{:S(2)}) %copy-start.1) | copy-done | bytes 393240
  2.8 0.0 copy-start.2
  2.8 0.9 %copy-done.2 = f32[192,128]{1,0:T(8,128)S(1)} copy-done((f32[192,128]{1,0:T(8,128)S(1)}, f32[192,128]{1,0:T(8,128)}, u32[]{:S(2)}) %copy-start.2) | copy-done | bytes 98328
  3.7 0.0 copy-start.3
  3.7 0.9 %copy-done.3 = s32[192,128]{1,0:T(8,128)S(1)} copy-done((s32[192,128]{1,0:T(8,128)S(1)}, s32[192,128]{1,0:T(8,128)}, u32[]{:S(2)}) %copy-start.3) | copy-done | bytes 98328
  4.5 2.4 %pack.1 = (f32[192,128]{1,0:T(8,128)S(1)}, f32[192,128]{1,0:T(8,128)S(1)}, f32[8,40,128]{2,1,0:T(8,128)}, f32[40,128]{1,0:T(8,128)S(1)}, f32[8,192,128]{2,1,0:T(...) custom-call(f32[8,192,128]{2,1,0:T(8,128)S(1)} %copy-done, ...), custom_call_target="tpu_custom_call" | custom-call | tf_op jit(solution)/shard_map/pack/pallas_call | solution.py:324
  7.0 6.4 %all-to-all-start = ((f32[8,40,128]{2,1,0:T(8,128)}), f32[8,40,128]{2,1,0:T(8,128)S(1)}, u32[]{:S(2)}, u32[]{:S(2)}) async-start(f32[8,40,128]{2,1,0:T(8,128)} %get-tuple-element.21), calls=%async_computation | async-start | bytes 327680 | tf_op jit(solution)/shard_map/all_to_all | solution.py:338
  13.3 0.5 collective-permute-start
  13.8 3.1 %collective-permute-start.1 = (f32[192,128]{1,0:T(8,128)S(1)}, f32[192,128]{1,0:T(8,128)S(1)}, u32[]{:S(2)}, u32[]{:S(2)}) collective-permute-start(f32[192,128]{1,0:T(8,128)S(1)} %get-tuple-element.19), channel_id=1, source_target_pairs={{0,7},{1,0},{2,1},{3,2},{4,3},{5,4},{6,5},{7,6},{8,15},{9,8},{10,9... | collective-permute-start | bytes 294920 | tf_op jit(solution)/shard_map/ppermute | solution.py:307
  16.9 0.7 %slice_bitcast_fusion = f32[40,128]{1,0:T(8,128)S(1)} fusion(f32[8,40,128]{2,1,0:T(8,128)} %get-tuple-element.21), kind=kLoop, calls=%fused_computation.2 | loop fusion | bytes 40960 | tf_op jit(solution)/shard_map/squeeze | solution.py:339
  17.6 4.9 %collective-permute-done.from_west = f32[192,128]{1,0:T(8,128)S(1)} collective-permute-done((f32[192,128]{1,0:T(8,128)S(1)}, f32[192,128]{1,0:T(8,128)S(1)}, u32[]{:S(2)}, u32[]{:S(2)}) %collective-permute-start) | collective-permute-done | bytes 98336 | tf_op jit(solution)/shard_map/ppermute | solution.py:307
  22.5 0.0 collective-permute-done.1.from_east
  22.5 1.3 %collective-permute-start.2 = (f32[48,128]{1,0:T(8,128)S(1)}, f32[48,128]{1,0:T(8,128)S(1)}, u32[]{:S(2)}, u32[]{:S(2)}) collective-permute-start(f32[48,128]{1,0:T(8,128)S(1)} %pad_maximum_fusion), channel_id=1, source_target_pairs={{8,0},{16,8},{24,16},{9,1},{17,9},{25,17},{10,2},{18,10},{26,18},{... | collective-permute-start | bytes 73736 | tf_op jit(solution)/shard_map/ppermute | solution.py:307
  23.8 0.0 copy-start.4
  23.9 4.5 %collective-permute-start.3 = (f32[48,128]{1,0:T(8,128)S(1)}, f32[48,128]{1,0:T(8,128)S(1)}, u32[]{:S(2)}, u32[]{:S(2)}) collective-permute-start(f32[48,128]{1,0:T(8,128)S(1)} %pad_maximum_fusion.1), channel_id=1, source_target_pairs={{0,8},{8,16},{16,24},{1,9},{9,17},{17,25},{2,10},{10,18},{18,26},{... | collective-permute-start | bytes 73736 | tf_op jit(solution)/shard_map/ppermute | solution.py:307
  28.4 0.0 collective-permute-done.2.from_north
  28.4 1.5 %collective-permute-done.3.from_south = f32[48,128]{1,0:T(8,128)S(1)} collective-permute-done((f32[48,128]{1,0:T(8,128)S(1)}, f32[48,128]{1,0:T(8,128)S(1)}, u32[]{:S(2)}, u32[]{:S(2)}) %collective-permute-start.3) | collective-permute-done | bytes 24608 | tf_op jit(solution)/shard_map/ppermute | solution.py:307
  29.9 0.0 all-to-all-done.ring
  29.9 0.0 copy-done.4
  29.9 13.6 %stencil.1 = (f32[8,192,128]{2,1,0:T(8,128)S(1)}, f32[8,192,128]{2,1,0:T(8,128)S(1)}, f32[8,192,128]{2,1,0:T(8,128)S(1)}, f32[32,8,128]{2,1,0:T(8,128)S(1)}) custom-call(s32[1024]{0:T(1024)S(1)} %copy-done.4, f32[8,192,128]{2,1,0:T(8,128)S(1)} %get-tuple-element.14.scaled.zeroth, f32[192,128]{1,0:T(8,128)S(1)} %get-tuple-element.15.weights, ...), custom_call_target="tpu_custom_call" | custom-call | tf_op jit(solution)/shard_map/stencil/pallas_call | solution.py:347
  43.5 13.0 %all_to_all.10.moments = f32[32,8,128]{2,1,0:T(8,128)S(1)} all-to-all(f32[32,8,128]{2,1,0:T(8,128)S(1)} %get-tuple-element.22), channel_id=1, replica_groups=mesh['lat'=4,'lon'=8] {'lat','lon'}, dimensions={0} | all-to-all | bytes 262144 | tf_op jit(solution)/shard_map/all_to_all | solution.py:362
  56.5 3.1 %combine.1 = (f32[8,192,128]{2,1,0:T(8,128)}, f32[8,192,128]{2,1,0:T(8,128)}) custom-call(f32[32,8,128]{2,1,0:T(8,128)S(1)} %all_to_all.10.moments, f32[8,192,128]{2,1,0:T(8,128)S(1)} %get-tuple-element.14.scaled.zeroth, f32[192,128]{1,0:T(8,128)S(1)} %get-tuple-element.17.center, f32[8,192,128]{2,1,0:T(8,128)S(1)} %get-tuple-element.23.first, ...), custom_call_target="tpu_custom_call" | custom-call | tf_op jit(solution)/shard_map/combine/pallas_call | solution.py:365
  (5 shorter events, 0.0 us)
Async XLA Ops:
  0.6 1.1 %copy-start = (f32[8,192,128]{2,1,0:T(8,128)S(1)}, f32[8,192,128]{2,1,0:T(8,128)}, u32[]{:S(2)}) copy-start(f32[8,192,128]{2,1,0:T(8,128)} %rhs.1) | copy-start | bytes 2359300
  1.8 1.0 %copy-start.1 = (f32[4,192,128]{2,1,0:T(8,128)S(1)}, f32[4,192,128]{2,1,0:T(8,128)}, u32[]{:S(2)}) copy-start(f32[4,192,128]{2,1,0:T(8,128)} %couplings.1) | copy-start | bytes 1179652
  2.8 0.9 %copy-start.2 = (f32[192,128]{1,0:T(8,128)S(1)}, f32[192,128]{1,0:T(8,128)}, u32[]{:S(2)}) copy-start(f32[192,128]{1,0:T(8,128)} %center.1) | copy-start | bytes 294916
  3.7 0.9 %copy-start.3 = (s32[192,128]{1,0:T(8,128)S(1)}, s32[192,128]{1,0:T(8,128)}, u32[]{:S(2)}) copy-start(s32[192,128]{1,0:T(8,128)} %land.1) | copy-start | bytes 294916
  7.0 22.9 %all-to-all-start = ((f32[8,40,128]{2,1,0:T(8,128)}), f32[8,40,128]{2,1,0:T(8,128)S(1)}, u32[]{:S(2)}, u32[]{:S(2)}) async-start(f32[8,40,128]{2,1,0:T(8,128)} %get-tuple-element.21), calls=%async_computation | async-start | bytes 327680 | tf_op jit(solution)/shard_map/all_to_all | solution.py:338
  13.3 9.2 %collective-permute-start = (f32[192,128]{1,0:T(8,128)S(1)}, f32[192,128]{1,0:T(8,128)S(1)}, u32[]{:S(2)}, u32[]{:S(2)}) collective-permute-start(f32[192,128]{1,0:T(8,128)S(1)} %get-tuple-element.18), channel_id=1, source_target_pairs={{0,1},{1,2},{2,3},{3,4},{4,5},{5,6},{6,7},{7,0},{8,9},{9,10},{10,1... | collective-permute-start | bytes 294920 | tf_op jit(solution)/shard_map/ppermute | solution.py:307
  13.8 8.7 %collective-permute-start.1 = (f32[192,128]{1,0:T(8,128)S(1)}, f32[192,128]{1,0:T(8,128)S(1)}, u32[]{:S(2)}, u32[]{:S(2)}) collective-permute-start(f32[192,128]{1,0:T(8,128)S(1)} %get-tuple-element.19), channel_id=1, source_target_pairs={{0,7},{1,0},{2,1},{3,2},{4,3},{5,4},{6,5},{7,6},{8,15},{9,8},{10,9... | collective-permute-start | bytes 294920 | tf_op jit(solution)/shard_map/ppermute | solution.py:307
  22.5 5.9 %collective-permute-start.2 = (f32[48,128]{1,0:T(8,128)S(1)}, f32[48,128]{1,0:T(8,128)S(1)}, u32[]{:S(2)}, u32[]{:S(2)}) collective-permute-start(f32[48,128]{1,0:T(8,128)S(1)} %pad_maximum_fusion), channel_id=1, source_target_pairs={{8,0},{16,8},{24,16},{9,1},{17,9},{25,17},{10,2},{18,10},{26,18},{... | collective-permute-start | bytes 73736 | tf_op jit(solution)/shard_map/ppermute | solution.py:307
  23.8 6.1 %copy-start.4 = (s32[1024]{0:T(1024)S(1)}, s32[1024]{0:T(1024)}, u32[]{:S(2)}) copy-start(s32[1024]{0:T(1024)} %partner.1) | copy-start | bytes 12292
  23.9 6.1 %collective-permute-start.3 = (f32[48,128]{1,0:T(8,128)S(1)}, f32[48,128]{1,0:T(8,128)S(1)}, u32[]{:S(2)}, u32[]{:S(2)}) collective-permute-start(f32[48,128]{1,0:T(8,128)S(1)} %pad_maximum_fusion.1), channel_id=1, source_target_pairs={{0,8},{8,16},{16,24},{1,9},{9,17},{17,25},{2,10},{10,18},{18,26},{... | collective-permute-start | bytes 73736 | tf_op jit(solution)/shard_map/ppermute | solution.py:307
where the time goes:
time: 60.1 us; the launch traced here: 59.6 us
  Pallas kernels  19.1 us (32%)
  starting transfers between devices  15.8 us (26%)
  blocking collectives  13 us (22%)
  waiting for transfers between devices  6.35 us (11%)
  local copies, waits for them, and re-layouts  4.64 us (8%)
  between operations  0.71 us (1%)
    pallas_call x1, Pallas kernels, body(): pl.pallas_call(stencil_kernel, in_specs=[smem] + [vmem] * 9, out_specs=[v...  13.6 us
    all_to_all x1, blocking collectives, body(): moments = lax.all_to_all(moments, ('lat', 'lon'), 0, 0, tiled=False)  13 us
    ppermute x4, starting transfers between devices, shifted(): return lax.ppermute(value, axis, pairs)  9.4 us
    all_to_all x1, starting transfers between devices, body(): ring = lax.all_to_all(north, 'lon', 0, 0, tiled=False)  6.37 us
    ppermute x4, waiting for transfers between devices, shifted(): return lax.ppermute(value, axis, pairs)  6.35 us
    unnamed x10, local copies, waits for them, and re-layouts  3.91 us
    pallas_call x1, Pallas kernels, body(): pl.pallas_call(combine_kernel, in_specs=[vmem] * 6, out_specs=[vmem] * 2,...  3.07 us
    pallas_call x1, Pallas kernels, body(): pl.pallas_call(pack_kernel, in_specs=[pl.BlockSpec(memory_space=pltpu.HBM...  2.42 us
  transfers between devices with their start and end apart: 5, of which 2 were waited for; matrix products, arithmetic and copies ran while one was open for 1% of the time, Pallas kernels for 0%

commit v1 on v0

--- a/solution.py
+++ b/solution.py
@@ -12,7 +12,7 @@
 
 
 def pack_kernel(
-    rhs, center, couplings, land, east, west, north, south, scaled, weights, edges, scale, mask, arrivals
+    rhs, center, couplings, land, east, west, spread_north, north, south, scaled, weights, edges, scale, mask, arrivals
 ):
     members = rhs.shape[0]
     fields = members + couplings.shape[0] + 1
@@ -52,8 +52,7 @@
         return carry
 
     lax.fori_loop(0, rows // SUB, step, 0, unroll=2)
-    copies = north.shape[0]
-    for ref, at in ((north.at[0], rows - DEPTH), (south, 0)):
+    for ref, at in ((north, rows - DEPTH), (south, 0)):
         span = slice(at, at + DEPTH)
         for f in range(fields):
             if f < members:
@@ -65,9 +64,9 @@
             ref[DEPTH * f : DEPTH * (f + 1), :] = value
         used = DEPTH * fields
         ref[used:, :] = jnp.zeros((ref.shape[0] - used, cols), jnp.float32)
-    top = north[0]
-    for b in range(1, copies):
-        north[b] = top
+    top = north[...]
+    for b in range(spread_north.shape[0]):
+        spread_north[b] = top
 
 
 def stencil_kernel(
@@ -251,7 +250,7 @@
         moments[b] = tile
 
 
-def combine_kernel(moments, zeroth, center, first, second, third, solution, residual):
+def combine_kernel(moments, zeroth, center, first, second, third, solution, residual, got, left, sent):
     def inner(p, q):
         total = 0.0
         for i, a in enumerate(p):
@@ -287,18 +286,23 @@
     wide_answer = [jnp.broadcast_to(a, (members, cols)) for a in answer]
     wide_scaled = [jnp.broadcast_to(a, (members, cols)) for a in scaled]
 
-    def chunk(index, carry):
-        here = pl.ds(pl.multiple_of(index * SUB, SUB), SUB)
-        scale = center[here, :]
-        for m in range(members):
+    copies = []
+    for m in range(members):
+
+        def chunk(index, carry):
+            here = pl.ds(pl.multiple_of(index * SUB, SUB), SUB)
             basis = [zeroth[m, here, :], first[m, here, :], second[m, here, :], third[m, here, :]]
-            got = sum(a[m : m + 1, :] * v for a, v in zip(wide_answer, basis))
-            left = sum(a[m : m + 1, :] * v for a, v in zip(wide_scaled, basis))
-            solution[m, here, :] = got
-            residual[m, here, :] = scale * left
-        return carry
-
-    lax.fori_loop(0, rows // SUB, chunk, 0)
+            got[m, here, :] = sum(a[m : m + 1, :] * v for a, v in zip(wide_answer, basis))
+            left[m, here, :] = center[here, :] * sum(a[m : m + 1, :] * v for a, v in zip(wide_scaled, basis))
+            return carry
+
+        lax.fori_loop(0, rows // SUB, chunk, 0, unroll=4)
+        for i, (kept, out) in enumerate(((got, solution), (left, residual))):
+            copy = pltpu.make_async_copy(kept.at[m], out.at[m], sent.at[i, m])
+            copy.start()
+            copies.append(copy)
+    for copy in copies:
+        copy.wait()
 
 
 def shifted(value, axis, by, closed):
@@ -321,22 +325,21 @@
 
     lon_count = lax.axis_size("lon")
     devices = lon_count * lax.axis_size("lat")
-    east, west, north, south, scaled, weights, edges, scale = pl.pallas_call(
+    east, west, spread_north, north, south, scaled, weights, edges, scale = pl.pallas_call(
         pack_kernel,
         in_specs=[pl.BlockSpec(memory_space=pltpu.HBM)] * 4,
-        out_specs=[vmem] * 8,
+        out_specs=[vmem] * 9,
         out_shape=[shape(rows, cols)] * 2
-        + [shape(lon_count, packed, cols), shape(packed, cols)]
+        + [shape(lon_count, packed, cols), shape(packed, cols), shape(packed, cols)]
         + [shape(members, rows, cols), shape(rows, cols), shape(*couplings.shape), shape(rows, cols)],
         scratch_shapes=[pltpu.VMEM((rows, cols), jnp.int32), pltpu.SemaphoreType.DMA((4,))],
         compiler_params=params,
         name="pack",
-    )(right_side, center, couplings, land_sea)
+    )(*(pltpu.with_memory_space_constraint(x, pltpu.HBM) for x in (right_side, center, couplings, land_sea)))
 
     from_west = shifted(east, "lon", 1, True)
     from_east = shifted(west, "lon", -1, True)
-    ring = lax.all_to_all(north, "lon", 0, 0, tiled=False)
-    north = north[0]
+    ring = lax.all_to_all(spread_north, "lon", 0, 0, tiled=False)
     in_west = (lax.broadcasted_iota(jnp.int32, (SUB, cols), 1) % (2 * DEPTH)) < DEPTH
     upper = jnp.where(in_west, from_west[rows - SUB :], from_east[rows - SUB :])
     lower = jnp.where(in_west, from_west[:SUB], from_east[:SUB])
@@ -365,8 +368,9 @@
         pl.pallas_call(
             combine_kernel,
             in_specs=[vmem] * 6,
-            out_specs=[vmem] * 2,
+            out_specs=[pl.BlockSpec(memory_space=pltpu.HBM)] * 2,
             out_shape=[shape(members, rows, cols)] * 2,
+            scratch_shapes=[pltpu.VMEM((members, rows, cols), f32)] * 2 + [pltpu.SemaphoreType.DMA((2, members))],
             compiler_params=params,
             name="combine",
         )(moments, scaled, scale, first, second, third)

time: 60.1 us -> 57 us (0.948)
  local copies, waits for them, and re-layouts: 4.64 us -> 0.01 us
  Pallas kernels: 19.1 us -> 20 us
  waiting for transfers between devices: 6.35 us -> 7.08 us
    unnamed x10 -> x2, local copies, waits for them, and re-layouts: 3.91 us -> 0.01 us
    pallas_call x1, Pallas kernels: 2.42 us -> 3.29 us  [body(): pl.pallas_call(pack_kernel, in_specs=[pl.BlockSpec(memory_space=pltpu.HBM...]
    ppermute x4, waiting for transfers between devices: 6.35 us -> 7.08 us  [shifted(): return lax.ppermute(value, axis, pairs)]
    squeeze x1 -> x0, local copies, waits for them, and re-layouts: 0.73 us -> none  [body(): north = north[0]]
  transfers between devices with their start and end apart: 5 -> 5, of which waited for: 2 -> 2; matrix products, arithmetic and copies ran while one was open for 1% -> 0% of each run, Pallas kernels for 0% -> 0%
where the time goes in v1:
time: 57 us; the launch traced here: 56.6 us
  Pallas kernels  20 us (35%)
  starting transfers between devices  15.8 us (28%)
  blocking collectives  13 us (23%)
  waiting for transfers between devices  7.08 us (12%)
  between operations  0.7 us (1%)
    pallas_call x1, Pallas kernels, body(): pl.pallas_call(stencil_kernel, in_specs=[smem] + [vmem] * 9, out_specs=[v...  13.6 us
    all_to_all x1, blocking collectives, body(): moments = lax.all_to_all(moments, ('lat', 'lon'), 0, 0, tiled=False)  13 us
    ppermute x4, starting transfers between devices, shifted(): return lax.ppermute(value, axis, pairs)  9.4 us
    ppermute x4, waiting for transfers between devices, shifted(): return lax.ppermute(value, axis, pairs)  7.08 us
    all_to_all x1, starting transfers between devices, body(): ring = lax.all_to_all(spread_north, 'lon', 0, 0, tiled=False)  6.37 us
    pallas_call x1, Pallas kernels, body(): pl.pallas_call(pack_kernel, in_specs=[pl.BlockSpec(memory_space=pltpu.HBM...  3.29 us
    pallas_call x1, Pallas kernels, body(): pl.pallas_call(combine_kernel, in_specs=[vmem] * 6, out_specs=[pl.BlockSp...  3.16 us
  transfers between devices with their start and end apart: 5, of which 2 were waited for; matrix products, arithmetic and copies ran while one was open for 0% of the time, Pallas kernels for 0%

profile of v1, /device:TPU:0, one launch (start us, length us, event | category | flops | bytes accessed | tf_op | source)
XLA Modules:
  0.0 56.6 jit_solution(18027977624410518858)
XLA Ops:
  0.6 3.3 %pack.1 = (f32[192,128]{1,0:T(8,128)S(1)}, f32[192,128]{1,0:T(8,128)S(1)}, f32[8,40,128]{2,1,0:T(8,128)}, f32[40,128]{1,0:T(8,128)S(1)}, f32[40,128]{1,0:T(8,128...) custom-call(f32[8,192,128]{2,1,0:T(8,128)} %rhs.1, ...), custom_call_target="tpu_custom_call" | custom-call | tf_op jit(solution)/shard_map/pack/pallas_call | solution.py:328
  3.9 6.4 %all-to-all-start = ((f32[8,40,128]{2,1,0:T(8,128)}), f32[8,40,128]{2,1,0:T(8,128)S(1)}, u32[]{:S(2)}, u32[]{:S(2)}) async-start(f32[8,40,128]{2,1,0:T(8,128)} %get-tuple-element.23), calls=%async_computation | async-start | bytes 327680 | tf_op jit(solution)/shard_map/all_to_all | solution.py:342
  10.3 0.5 collective-permute-start
  10.8 3.1 %collective-permute-start.1 = (f32[192,128]{1,0:T(8,128)S(1)}, f32[192,128]{1,0:T(8,128)S(1)}, u32[]{:S(2)}, u32[]{:S(2)}) collective-permute-start(f32[192,128]{1,0:T(8,128)S(1)} %get-tuple-element.20), channel_id=1, source_target_pairs={{0,7},{1,0},{2,1},{3,2},{4,3},{5,4},{6,5},{7,6},{8,15},{9,8},{10,9... | collective-permute-start | bytes 294920 | tf_op jit(solution)/shard_map/ppermute | solution.py:311
  13.9 5.6 %collective-permute-done.from_west = f32[192,128]{1,0:T(8,128)S(1)} collective-permute-done((f32[192,128]{1,0:T(8,128)S(1)}, f32[192,128]{1,0:T(8,128)S(1)}, u32[]{:S(2)}, u32[]{:S(2)}) %collective-permute-start) | collective-permute-done | bytes 98336 | tf_op jit(solution)/shard_map/ppermute | solution.py:311
  19.5 0.0 collective-permute-done.1.from_east
  19.5 1.3 %collective-permute-start.2 = (f32[48,128]{1,0:T(8,128)S(1)}, f32[48,128]{1,0:T(8,128)S(1)}, u32[]{:S(2)}, u32[]{:S(2)}) collective-permute-start(f32[48,128]{1,0:T(8,128)S(1)} %pad_maximum_fusion), channel_id=1, source_target_pairs={{8,0},{16,8},{24,16},{9,1},{17,9},{25,17},{10,2},{18,10},{26,18},{... | collective-permute-start | bytes 73736 | tf_op jit(solution)/shard_map/ppermute | solution.py:311
  20.8 0.0 copy-start
  20.8 4.5 %collective-permute-start.3 = (f32[48,128]{1,0:T(8,128)S(1)}, f32[48,128]{1,0:T(8,128)S(1)}, u32[]{:S(2)}, u32[]{:S(2)}) collective-permute-start(f32[48,128]{1,0:T(8,128)S(1)} %pad_maximum_fusion.1), channel_id=1, source_target_pairs={{0,8},{8,16},{16,24},{1,9},{9,17},{17,25},{2,10},{10,18},{18,26},{... | collective-permute-start | bytes 73736 | tf_op jit(solution)/shard_map/ppermute | solution.py:311
  25.4 0.0 collective-permute-done.2.from_north
  25.4 1.5 %collective-permute-done.3.from_south = f32[48,128]{1,0:T(8,128)S(1)} collective-permute-done((f32[48,128]{1,0:T(8,128)S(1)}, f32[48,128]{1,0:T(8,128)S(1)}, u32[]{:S(2)}, u32[]{:S(2)}) %collective-permute-start.3) | collective-permute-done | bytes 24608 | tf_op jit(solution)/shard_map/ppermute | solution.py:311
  26.9 0.0 all-to-all-done.ring
  26.9 0.0 copy-done
  26.9 13.6 %stencil.1 = (f32[8,192,128]{2,1,0:T(8,128)S(1)}, f32[8,192,128]{2,1,0:T(8,128)S(1)}, f32[8,192,128]{2,1,0:T(8,128)S(1)}, f32[32,8,128]{2,1,0:T(8,128)S(1)}) custom-call(s32[1024]{0:T(1024)S(1)} %copy-done, f32[8,192,128]{2,1,0:T(8,128)S(1)} %get-tuple-element.15.scaled.zeroth, f32[192,128]{1,0:T(8,128)S(1)} %get-tuple-element.16.weights, ...), custom_call_target="tpu_custom_call" | custom-call | tf_op jit(solution)/shard_map/stencil/pallas_call | solution.py:350
  40.5 13.0 %all_to_all.10.moments = f32[32,8,128]{2,1,0:T(8,128)S(1)} all-to-all(f32[32,8,128]{2,1,0:T(8,128)S(1)} %get-tuple-element.24), channel_id=1, replica_groups=mesh['lat'=4,'lon'=8] {'lat','lon'}, dimensions={0} | all-to-all | bytes 262144 | tf_op jit(solution)/shard_map/all_to_all | solution.py:365
  53.5 3.2 %combine.1 = (f32[8,192,128]{2,1,0:T(8,128)}, f32[8,192,128]{2,1,0:T(8,128)}) custom-call(f32[32,8,128]{2,1,0:T(8,128)S(1)} %all_to_all.10.moments, f32[8,192,128]{2,1,0:T(8,128)S(1)} %get-tuple-element.15.scaled.zeroth, f32[192,128]{1,0:T(8,128)S(1)} %get-tuple-element.18.center, f32[8,192,128]{2,1,0:T(8,128)S(1)} %get-tuple-element.25.first, ...), custom_call_target="tpu_custom_call" | custom-call | tf_op jit(solution)/shard_map/combine/pallas_call | solution.py:368
  (5 shorter events, 0.0 us)
Async XLA Ops:
  3.9 22.9 %all-to-all-start = ((f32[8,40,128]{2,1,0:T(8,128)}), f32[8,40,128]{2,1,0:T(8,128)S(1)}, u32[]{:S(2)}, u32[]{:S(2)}) async-start(f32[8,40,128]{2,1,0:T(8,128)} %get-tuple-element.23), calls=%async_computation | async-start | bytes 327680 | tf_op jit(solution)/shard_map/all_to_all | solution.py:342
  10.3 9.2 %collective-permute-start = (f32[192,128]{1,0:T(8,128)S(1)}, f32[192,128]{1,0:T(8,128)S(1)}, u32[]{:S(2)}, u32[]{:S(2)}) collective-permute-start(f32[192,128]{1,0:T(8,128)S(1)} %get-tuple-element.19), channel_id=1, source_target_pairs={{0,1},{1,2},{2,3},{3,4},{4,5},{5,6},{6,7},{7,0},{8,9},{9,10},{10,1... | collective-permute-start | bytes 294920 | tf_op jit(solution)/shard_map/ppermute | solution.py:311
  10.8 8.7 %collective-permute-start.1 = (f32[192,128]{1,0:T(8,128)S(1)}, f32[192,128]{1,0:T(8,128)S(1)}, u32[]{:S(2)}, u32[]{:S(2)}) collective-permute-start(f32[192,128]{1,0:T(8,128)S(1)} %get-tuple-element.20), channel_id=1, source_target_pairs={{0,7},{1,0},{2,1},{3,2},{4,3},{5,4},{6,5},{7,6},{8,15},{9,8},{10,9... | collective-permute-start | bytes 294920 | tf_op jit(solution)/shard_map/ppermute | solution.py:311
  19.5 5.9 %collective-permute-start.2 = (f32[48,128]{1,0:T(8,128)S(1)}, f32[48,128]{1,0:T(8,128)S(1)}, u32[]{:S(2)}, u32[]{:S(2)}) collective-permute-start(f32[48,128]{1,0:T(8,128)S(1)} %pad_maximum_fusion), channel_id=1, source_target_pairs={{8,0},{16,8},{24,16},{9,1},{17,9},{25,17},{10,2},{18,10},{26,18},{... | collective-permute-start | bytes 73736 | tf_op jit(solution)/shard_map/ppermute | solution.py:311
  20.8 6.1 %copy-start = (s32[1024]{0:T(1024)S(1)}, s32[1024]{0:T(1024)}, u32[]{:S(2)}) copy-start(s32[1024]{0:T(1024)} %partner.1) | copy-start | bytes 12292
  20.8 6.1 %collective-permute-start.3 = (f32[48,128]{1,0:T(8,128)S(1)}, f32[48,128]{1,0:T(8,128)S(1)}, u32[]{:S(2)}, u32[]{:S(2)}) collective-permute-start(f32[48,128]{1,0:T(8,128)S(1)} %pad_maximum_fusion.1), channel_id=1, source_target_pairs={{0,8},{8,16},{16,24},{1,9},{9,17},{17,25},{2,10},{10,18},{18,26},{... | collective-permute-start | bytes 73736 | tf_op jit(solution)/shard_map/ppermute | solution.py:311

commit v2 on v1

--- a/solution.py
+++ b/solution.py
@@ -51,7 +51,7 @@
         west[here, :] = to_west
         return carry
 
-    lax.fori_loop(0, rows // SUB, step, 0, unroll=2)
+    lax.fori_loop(0, rows // SUB, step, 0, unroll=4)
     for ref, at in ((north, rows - DEPTH), (south, 0)):
         span = slice(at, at + DEPTH)
         for f in range(fields):
@@ -115,7 +115,7 @@
             held[f, pl.ds(to, SUB), cols:] = spread(side, f)
         return carry
 
-    lax.fori_loop(0, rows // SUB, fill, 0)
+    lax.fori_loop(0, rows // SUB, fill, 0, unroll=4)
 
     side_south = from_south[packed : packed + SUB, :]
     for f in range(fields):
@@ -199,7 +199,7 @@
     is_first = wide_row == 0
     is_last = wide_row == SUB - 1
     chunks = rows // SUB
-    lax.fori_loop(1, chunks + 3, make_coeff, 0)
+    lax.fori_loop(1, chunks + 3, make_coeff, 0, unroll=2)
 
     def level(source, target, result):
         def chunk(index, carry, inside):

time: 57 us -> 54.4 us (0.954)
  Pallas kernels: 20 us -> 17.5 us
    pallas_call x1, Pallas kernels: 13.6 us -> 11.5 us  [body(): pl.pallas_call(stencil_kernel, in_specs=[smem] + [vmem] * 9, out_specs=[v...]
where the time goes in v2:
time: 54.4 us; the launch traced here: 54.1 us
  Pallas kernels  17.5 us (32%)
  starting transfers between devices  15.8 us (29%)
  blocking collectives  13 us (24%)
  waiting for transfers between devices  7.08 us (13%)
  between operations  0.7 us (1%)
    all_to_all x1, blocking collectives, body(): moments = lax.all_to_all(moments, ('lat', 'lon'), 0, 0, tiled=False)  13 us
    pallas_call x1, Pallas kernels, body(): pl.pallas_call(stencil_kernel, in_specs=[smem] + [vmem] * 9, out_specs=[v...  11.5 us
    ppermute x4, starting transfers between devices, shifted(): return lax.ppermute(value, axis, pairs)  9.4 us
    ppermute x4, waiting for transfers between devices, shifted(): return lax.ppermute(value, axis, pairs)  7.08 us
    all_to_all x1, starting transfers between devices, body(): ring = lax.all_to_all(spread_north, 'lon', 0, 0, tiled=False)  6.37 us
    pallas_call x1, Pallas kernels, body(): pl.pallas_call(combine_kernel, in_specs=[vmem] * 6, out_specs=[pl.BlockSp...  3.16 us
    pallas_call x1, Pallas kernels, body(): pl.pallas_call(pack_kernel, in_specs=[pl.BlockSpec(memory_space=pltpu.HBM...  2.82 us
  transfers between devices with their start and end apart: 5, of which 2 were waited for; matrix products, arithmetic and copies ran while one was open for 0% of the time, Pallas kernels for 0%

profile of v2, /device:TPU:0, one launch (start us, length us, event | category | flops | bytes accessed | tf_op | source)
XLA Modules:
  0.0 54.1 jit_solution(4529733513857889103)
XLA Ops:
  0.6 2.8 %pack.1 = (f32[192,128]{1,0:T(8,128)S(1)}, f32[192,128]{1,0:T(8,128)S(1)}, f32[8,40,128]{2,1,0:T(8,128)}, f32[40,128]{1,0:T(8,128)S(1)}, f32[40,128]{1,0:T(8,128...) custom-call(f32[8,192,128]{2,1,0:T(8,128)} %rhs.1, ...), custom_call_target="tpu_custom_call" | custom-call | tf_op jit(solution)/shard_map/pack/pallas_call | solution.py:328
  3.5 6.4 %all-to-all-start = ((f32[8,40,128]{2,1,0:T(8,128)}), f32[8,40,128]{2,1,0:T(8,128)S(1)}, u32[]{:S(2)}, u32[]{:S(2)}) async-start(f32[8,40,128]{2,1,0:T(8,128)} %get-tuple-element.23), calls=%async_computation | async-start | bytes 327680 | tf_op jit(solution)/shard_map/all_to_all | solution.py:342
  9.8 0.5 collective-permute-start
  10.3 3.1 %collective-permute-start.1 = (f32[192,128]{1,0:T(8,128)S(1)}, f32[192,128]{1,0:T(8,128)S(1)}, u32[]{:S(2)}, u32[]{:S(2)}) collective-permute-start(f32[192,128]{1,0:T(8,128)S(1)} %get-tuple-element.20), channel_id=1, source_target_pairs={{0,7},{1,0},{2,1},{3,2},{4,3},{5,4},{6,5},{7,6},{8,15},{9,8},{10,9... | collective-permute-start | bytes 294920 | tf_op jit(solution)/shard_map/ppermute | solution.py:311
  13.4 5.6 %collective-permute-done.from_west = f32[192,128]{1,0:T(8,128)S(1)} collective-permute-done((f32[192,128]{1,0:T(8,128)S(1)}, f32[192,128]{1,0:T(8,128)S(1)}, u32[]{:S(2)}, u32[]{:S(2)}) %collective-permute-start) | collective-permute-done | bytes 98336 | tf_op jit(solution)/shard_map/ppermute | solution.py:311
  19.0 0.0 collective-permute-done.1.from_east
  19.0 1.3 %collective-permute-start.2 = (f32[48,128]{1,0:T(8,128)S(1)}, f32[48,128]{1,0:T(8,128)S(1)}, u32[]{:S(2)}, u32[]{:S(2)}) collective-permute-start(f32[48,128]{1,0:T(8,128)S(1)} %pad_maximum_fusion), channel_id=1, source_target_pairs={{8,0},{16,8},{24,16},{9,1},{17,9},{25,17},{10,2},{18,10},{26,18},{... | collective-permute-start | bytes 73736 | tf_op jit(solution)/shard_map/ppermute | solution.py:311
  20.3 0.0 copy-start
  20.3 4.5 %collective-permute-start.3 = (f32[48,128]{1,0:T(8,128)S(1)}, f32[48,128]{1,0:T(8,128)S(1)}, u32[]{:S(2)}, u32[]{:S(2)}) collective-permute-start(f32[48,128]{1,0:T(8,128)S(1)} %pad_maximum_fusion.1), channel_id=1, source_target_pairs={{0,8},{8,16},{16,24},{1,9},{9,17},{17,25},{2,10},{10,18},{18,26},{... | collective-permute-start | bytes 73736 | tf_op jit(solution)/shard_map/ppermute | solution.py:311
  24.9 0.0 collective-permute-done.2.from_north
  24.9 1.5 %collective-permute-done.3.from_south = f32[48,128]{1,0:T(8,128)S(1)} collective-permute-done((f32[48,128]{1,0:T(8,128)S(1)}, f32[48,128]{1,0:T(8,128)S(1)}, u32[]{:S(2)}, u32[]{:S(2)}) %collective-permute-start.3) | collective-permute-done | bytes 24608 | tf_op jit(solution)/shard_map/ppermute | solution.py:311
  26.4 0.0 all-to-all-done.ring
  26.4 0.0 copy-done
  26.4 11.5 %stencil.1 = (f32[8,192,128]{2,1,0:T(8,128)S(1)}, f32[8,192,128]{2,1,0:T(8,128)S(1)}, f32[8,192,128]{2,1,0:T(8,128)S(1)}, f32[32,8,128]{2,1,0:T(8,128)S(1)}) custom-call(s32[1024]{0:T(1024)S(1)} %copy-done, f32[8,192,128]{2,1,0:T(8,128)S(1)} %get-tuple-element.15.scaled.zeroth, f32[192,128]{1,0:T(8,128)S(1)} %get-tuple-element.16.weights, ...), custom_call_target="tpu_custom_call" | custom-call | tf_op jit(solution)/shard_map/stencil/pallas_call | solution.py:350
  37.9 13.0 %all_to_all.10.moments = f32[32,8,128]{2,1,0:T(8,128)S(1)} all-to-all(f32[32,8,128]{2,1,0:T(8,128)S(1)} %get-tuple-element.24), channel_id=1, replica_groups=mesh['lat'=4,'lon'=8] {'lat','lon'}, dimensions={0} | all-to-all | bytes 262144 | tf_op jit(solution)/shard_map/all_to_all | solution.py:365
  50.9 3.2 %combine.1 = (f32[8,192,128]{2,1,0:T(8,128)}, f32[8,192,128]{2,1,0:T(8,128)}) custom-call(f32[32,8,128]{2,1,0:T(8,128)S(1)} %all_to_all.10.moments, f32[8,192,128]{2,1,0:T(8,128)S(1)} %get-tuple-element.15.scaled.zeroth, f32[192,128]{1,0:T(8,128)S(1)} %get-tuple-element.18.center, f32[8,192,128]{2,1,0:T(8,128)S(1)} %get-tuple-element.25.first, ...), custom_call_target="tpu_custom_call" | custom-call | tf_op jit(solution)/shard_map/combine/pallas_call | solution.py:368
  (5 shorter events, 0.0 us)
Async XLA Ops:
  3.5 22.9 %all-to-all-start = ((f32[8,40,128]{2,1,0:T(8,128)}), f32[8,40,128]{2,1,0:T(8,128)S(1)}, u32[]{:S(2)}, u32[]{:S(2)}) async-start(f32[8,40,128]{2,1,0:T(8,128)} %get-tuple-element.23), calls=%async_computation | async-start | bytes 327680 | tf_op jit(solution)/shard_map/all_to_all | solution.py:342
  9.8 9.2 %collective-permute-start = (f32[192,128]{1,0:T(8,128)S(1)}, f32[192,128]{1,0:T(8,128)S(1)}, u32[]{:S(2)}, u32[]{:S(2)}) collective-permute-start(f32[192,128]{1,0:T(8,128)S(1)} %get-tuple-element.19), channel_id=1, source_target_pairs={{0,1},{1,2},{2,3},{3,4},{4,5},{5,6},{6,7},{7,0},{8,9},{9,10},{10,1... | collective-permute-start | bytes 294920 | tf_op jit(solution)/shard_map/ppermute | solution.py:311
  10.3 8.7 %collective-permute-start.1 = (f32[192,128]{1,0:T(8,128)S(1)}, f32[192,128]{1,0:T(8,128)S(1)}, u32[]{:S(2)}, u32[]{:S(2)}) collective-permute-start(f32[192,128]{1,0:T(8,128)S(1)} %get-tuple-element.20), channel_id=1, source_target_pairs={{0,7},{1,0},{2,1},{3,2},{4,3},{5,4},{6,5},{7,6},{8,15},{9,8},{10,9... | collective-permute-start | bytes 294920 | tf_op jit(solution)/shard_map/ppermute | solution.py:311
  19.0 5.9 %collective-permute-start.2 = (f32[48,128]{1,0:T(8,128)S(1)}, f32[48,128]{1,0:T(8,128)S(1)}, u32[]{:S(2)}, u32[]{:S(2)}) collective-permute-start(f32[48,128]{1,0:T(8,128)S(1)} %pad_maximum_fusion), channel_id=1, source_target_pairs={{8,0},{16,8},{24,16},{9,1},{17,9},{25,17},{10,2},{18,10},{26,18},{... | collective-permute-start | bytes 73736 | tf_op jit(solution)/shard_map/ppermute | solution.py:311
  20.3 6.1 %copy-start = (s32[1024]{0:T(1024)S(1)}, s32[1024]{0:T(1024)}, u32[]{:S(2)}) copy-start(s32[1024]{0:T(1024)} %partner.1) | copy-start | bytes 12292
  20.3 6.1 %collective-permute-start.3 = (f32[48,128]{1,0:T(8,128)S(1)}, f32[48,128]{1,0:T(8,128)S(1)}, u32[]{:S(2)}, u32[]{:S(2)}) collective-permute-start(f32[48,128]{1,0:T(8,128)S(1)} %pad_maximum_fusion.1), channel_id=1, source_target_pairs={{0,8},{8,16},{16,24},{1,9},{9,17},{17,25},{2,10},{10,18},{18,26},{... | collective-permute-start | bytes 73736 | tf_op jit(solution)/shard_map/ppermute | solution.py:311
